TPU v7x, 32 devices: a whole 2x2x4 slice. The times are simulated.
32 devices in a mesh: row: 4 (over y, x), col: 8 (over z, core).
Axes of the slice: x: 2, y: 2, z: 4, core: 2. Of those that a mesh axis runs over, the one named last changes fastest.
Arguments:
- docs: bfloat16 [4096, 4, 896], P(('row', 'col')), may hold values from -6 to 6
- routes: int32 [4096, 1], P(('row', 'col')), may hold values from 0 to 31; in each aligned block of 128 rows (0 to 127, 128 to 255, ...) at most 8 rows name the same one
- level_one: float32 [4, 896, 896], P('row', 'col'), may hold values from -6 to 6
- level_two: float32 [8, 896, 896], P('col', 'row'), may hold values from -6 to 6
- moment_one: float32 [4, 896, 896], P('row', 'col'), may hold values from -18 to 18
- moment_two: float32 [8, 896, 896], P('col', 'row'), may hold values from -18 to 18
Outputs:
- new_one: float32 [4, 896, 896], P('row', 'col')
- new_two: float32 [8, 896, 896], P('col', 'row')
- next_moment_one: float32 [4, 896, 896], P('row', 'col')
- next_moment_two: float32 [8, 896, 896], P('col', 'row')
Inputs may be any that keep to these rules, and one draw needn't show every extreme that they name: `routes`: each block names one path; among the 128 blocks of one device no path is named more than 8 times, and every path is named by some block.
All inputs are finite; a program needn't handle non-finite values.
Results may differ from a plain program's by a relative error of at most 0.017.
Values may be sent and summed in bfloat16 or wider, within the bound.
A program may use at most 128 MiB of HBM per device.

v0:
```python
import functools

import jax
import jax.numpy as jnp
from jax import lax
from jax.experimental import pallas as pl
from jax.experimental.pallas import tpu as pltpu
from jax.sharding import PartitionSpec as P

STEPS = 3


inner_rate = 64.0
outer_rate = 0.7
momentum_decay = 0.9

MESH = pl.DeviceIdType.MESH


def normalize(values):
    return values * lax.rsqrt(jnp.mean(values * values, axis=-1, keepdims=True) + 1e-06)


def path_loss(weights, inputs, targets, total):
    first, second = weights
    factor = inputs.shape[-1] ** (-0.5)
    hidden_in = (
        jnp.dot(
            normalize(inputs).astype(jnp.bfloat16),
            first.astype(jnp.bfloat16),
            preferred_element_type=jnp.float32,
        )
        * factor
    )
    hidden = inputs + jax.nn.silu(hidden_in)
    output = (
        hidden
        + jnp.dot(
            normalize(hidden).astype(jnp.bfloat16),
            second.astype(jnp.bfloat16),
            preferred_element_type=jnp.float32,
        )
        * factor
    )
    error = output - targets
    return 0.5 * jnp.sum(error * error) / total


def train_path(first, second, inputs, targets, total):
    for turn in range(STEPS):
        grads = jax.grad(path_loss)((first, second), inputs, targets, total)
        first = first - inner_rate * grads[0]
        second = second - inner_rate * grads[1]
    return (first, second)


def exchange_kernel(
    n_row, n_col, out_ref, cnt_ref, one_ref, two_ref,
    arrived, counts, whole_one, whole_two,
    doc_send, doc_recv, cnt_send, cnt_recv, up_send, down_send, one_recv,
    pair_send, pair_recv, two_send, two_recv, local_sem,
):
    row, col = lax.axis_index("row"), lax.axis_index("col")
    n = n_row * n_col
    me = row * n_col + col
    chips = n_col // 2
    place, core = col // 2, col % 2

    def device(index):
        return {"row": index // n_col, "col": index % n_col}

    barrier = pltpu.get_barrier_semaphore()

    def greet(k, carry):
        pl.semaphore_signal(
            barrier, inc=1, device_id=device((me + k) % n), device_id_type=MESH
        )
        return carry

    lax.fori_loop(1, n, greet, 0)
    own = [
        pltpu.make_async_copy(out_ref.at[me], arrived.at[me], local_sem.at[0]),
        pltpu.make_async_copy(cnt_ref.at[me], counts.at[me], local_sem.at[1]),
        pltpu.make_async_copy(one_ref, whole_one.at[col], local_sem.at[2]),
        pltpu.make_async_copy(two_ref, whole_two.at[row], local_sem.at[3]),
    ]
    for copy in own:
        copy.start()
    pl.semaphore_wait(barrier, n - 1)

    def along(source, block, to, send):
        return pltpu.make_async_remote_copy(
            src_ref=source,
            dst_ref=whole_one.at[block],
            send_sem=send.at[block],
            recv_sem=one_recv.at[block],
            device_id={"row": row, "col": to},
            device_id_type=MESH,
        )

    def across(source, block):
        return pltpu.make_async_remote_copy(
            src_ref=source,
            dst_ref=whole_one.at[block],
            send_sem=pair_send.at[block],
            recv_sem=pair_recv.at[block],
            device_id={"row": row, "col": place * 2 + 1 - core},
            device_id_type=MESH,
        )

    @pl.when(place < chips - 1)
    def _():
        along(one_ref, col, col + 2, up_send).start()

    @pl.when(place > 0)
    def _():
        along(one_ref, col, col - 2, down_send).start()

    across(one_ref, col).start()

    def two_copy(k):
        to = (row + k) % n_row
        return pltpu.make_async_remote_copy(
            src_ref=two_ref,
            dst_ref=whole_two.at[row],
            send_sem=two_send.at[k],
            recv_sem=two_recv.at[k],
            device_id={"row": to, "col": col},
            device_id_type=MESH,
        )

    def doc_copy(k):
        to = (me + k) % n
        return pltpu.make_async_remote_copy(
            src_ref=out_ref.at[to],
            dst_ref=arrived.at[me],
            send_sem=doc_send.at[k],
            recv_sem=doc_recv.at[k],
            device_id=device(to),
            device_id_type=MESH,
        )

    def cnt_copy(k):
        to = (me + k) % n
        return pltpu.make_async_remote_copy(
            src_ref=cnt_ref.at[to],
            dst_ref=counts.at[me],
            send_sem=cnt_send.at[k],
            recv_sem=cnt_recv.at[k],
            device_id=device(to),
            device_id_type=MESH,
        )

    def send_docs(low, high):
        def body(k, carry):
            doc_copy(k).start()
            cnt_copy(k).start()
            return carry

        lax.fori_loop(low, high, body, 0)

    def send_two(k, carry):
        two_copy(k).start()
        return carry

    lax.fori_loop(1, n_row, send_two, 0)
    cuts = [1 + (n - 1) * i // (chips - 1) for i in range(chips)]
    for step in range(1, chips):
        send_docs(cuts[step - 1], cuts[step])
        low, high = col - 2 * step, col + 2 * step

        @pl.when(place >= step)
        def _():
            along(one_ref, low, col, up_send).wait_recv()
            across(whole_one.at[low], low).start()

        @pl.when((place >= step) & (place < chips - 1))
        def _():
            along(whole_one.at[low], low, col + 2, up_send).start()

        @pl.when(place < chips - step)
        def _():
            along(one_ref, high, col, down_send).wait_recv()
            across(whole_one.at[high], high).start()

        @pl.when((place < chips - step) & (place > 0))
        def _():
            along(whole_one.at[high], high, col - 2, down_send).start()

    for copy in own:
        copy.wait()

    for q in range(chips):
        block = 2 * q + core
        across(one_ref, block).wait_send()
        across(one_ref, 2 * q + 1 - core).wait_recv()

        @pl.when((place >= q) & (place < chips - 1))
        def _():
            along(one_ref, block, col + 2, up_send).wait_send()

        @pl.when((place <= q) & (place > 0))
        def _():
            along(one_ref, block, col - 2, down_send).wait_send()

    def end_two(k, carry):
        two_copy(k).wait()
        return carry

    lax.fori_loop(1, n_row, end_two, 0)

    def end_docs(k, carry):
        doc_copy(k).wait()
        cnt_copy(k).wait()
        return carry

    lax.fori_loop(1, n, end_docs, 0)


def exchange(n_row, n_col, outgoing, tallies, level_one, level_two):
    n = n_row * n_col
    vmem = pl.BlockSpec(memory_space=pltpu.VMEM)
    dma = pltpu.SemaphoreType.DMA
    return pl.pallas_call(
        functools.partial(exchange_kernel, n_row, n_col),
        out_shape=(
            jax.ShapeDtypeStruct(outgoing.shape, outgoing.dtype),
            jax.ShapeDtypeStruct(tallies.shape, tallies.dtype),
            jax.ShapeDtypeStruct((n_col,) + level_one.shape, level_one.dtype),
            jax.ShapeDtypeStruct((n_row,) + level_two.shape, level_two.dtype),
        ),
        in_specs=[vmem] * 4,
        out_specs=(vmem,) * 4,
        scratch_shapes=[
            dma((n,)), dma((n,)), dma((n,)), dma((n,)),
            dma((n_col,)), dma((n_col,)), dma((n_col,)), dma((n_col,)), dma((n_col,)),
            dma((n_row,)), dma((n_row,)), dma((4,)),
        ],
        compiler_params=pltpu.CompilerParams(collective_id=0, has_side_effects=True),
    )(outgoing, tallies, level_one, level_two)


def scatter_kernel(
    n_row, n_col, one_ref, two_ref, share_one, share_two,
    pair_buf, part_buf, one_buf, two_buf,
    pair_send, pair_recv, one_send, one_recv, two_send, two_recv,
):
    row, col = lax.axis_index("row"), lax.axis_index("col")
    chips = n_col // 2
    place, core = col // 2, col % 2
    barrier = pltpu.get_barrier_semaphore()

    def greet(to_row, to_col):
        pl.semaphore_signal(
            barrier, inc=1, device_id={"row": to_row, "col": to_col}, device_id_type=MESH
        )

    partner = place * 2 + 1 - core
    greet(row, partner)
    for k in range(1, chips):
        greet(row, (col + 2 * k) % n_col)
    for k in range(1, n_row):
        greet((row + k) % n_row, col)
    pl.semaphore_wait(barrier, chips + n_row - 1)

    def pair_copy(q):
        return pltpu.make_async_remote_copy(
            src_ref=one_ref.at[2 * q + 1 - core],
            dst_ref=pair_buf.at[q],
            send_sem=pair_send.at[q],
            recv_sem=pair_recv.at[q],
            device_id={"row": row, "col": partner},
            device_id_type=MESH,
        )

    def two_copy(k):
        to = (row + k) % n_row
        return pltpu.make_async_remote_copy(
            src_ref=two_ref.at[to],
            dst_ref=two_buf.at[k],
            send_sem=two_send.at[k],
            recv_sem=two_recv.at[k],
            device_id={"row": to, "col": col},
            device_id_type=MESH,
        )

    def one_copy(k):
        return pltpu.make_async_remote_copy(
            src_ref=part_buf.at[k],
            dst_ref=one_buf.at[k],
            send_sem=one_send.at[k],
            recv_sem=one_recv.at[k],
            device_id={"row": row, "col": (col + 2 * k) % n_col},
            device_id_type=MESH,
        )

    for k in range(1, chips):
        pair_copy((place + k) % chips).start()
    pair_copy(place).start()
    for k in range(1, n_row):
        two_copy(k).start()
    for k in range(1, chips):
        q = (place + k) % chips
        pair_copy(q).wait_recv()
        part_buf[k] = (
            one_ref[2 * q + core].astype(jnp.float32) + pair_buf[q].astype(jnp.float32)
        ).astype(jnp.bfloat16)
        one_copy(k).start()
    pair_copy(place).wait_recv()
    share_one[...] = one_ref[col].astype(jnp.float32) + pair_buf[place].astype(jnp.float32)
    share_two[...] = two_ref[row].astype(jnp.float32)
    for k in range(1, chips):
        one_copy(k).wait_recv()
        share_one[...] += one_buf[k].astype(jnp.float32)
    for k in range(1, n_row):
        two_copy(k).wait_recv()
        share_two[...] += two_buf[k].astype(jnp.float32)
    for q in range(chips):
        pair_copy(q).wait_send()
    for k in range(1, chips):
        one_copy(k).wait_send()
    for k in range(1, n_row):
        two_copy(k).wait_send()


def scatter(n_row, n_col, change_one, change_two):
    width = change_one.shape[-1]
    chips = n_col // 2
    rows_one, rows_two = width // n_col, width // n_row
    vmem = pl.BlockSpec(memory_space=pltpu.VMEM)
    dma = pltpu.SemaphoreType.DMA
    return pl.pallas_call(
        functools.partial(scatter_kernel, n_row, n_col),
        out_shape=(
            jax.ShapeDtypeStruct((rows_one, width), jnp.float32),
            jax.ShapeDtypeStruct((rows_two, width), jnp.float32),
        ),
        in_specs=[vmem] * 2,
        out_specs=(vmem,) * 2,
        scratch_shapes=[
            pltpu.VMEM((chips, rows_one, width), jnp.bfloat16),
            pltpu.VMEM((chips, rows_one, width), jnp.bfloat16),
            pltpu.VMEM((chips, rows_one, width), jnp.bfloat16),
            pltpu.VMEM((n_row, rows_two, width), jnp.bfloat16),
            dma((chips,)), dma((chips,)), dma((chips,)), dma((chips,)),
            dma((n_row,)), dma((n_row,)),
        ],
        compiler_params=pltpu.CompilerParams(collective_id=1, has_side_effects=True),
    )(
        change_one.reshape(n_col, rows_one, width),
        change_two.reshape(n_row, rows_two, width),
    )


def shards(docs, routes, level_one, level_two, moment_one, moment_two):
    n_row = lax.axis_size("row")
    n_col = lax.axis_size("col")
    paths = n_row * n_col
    count = docs.shape[0]
    length = docs.shape[1]
    width = docs.shape[2]
    capacity = max(2, (2 * count + paths - 1) // paths)
    target = routes[:, 0]
    places = jnp.arange(count, dtype=jnp.int32)
    same = (target[:, None] == target[None, :]) & (places[None, :] < places[:, None])
    rank = jnp.sum(same.astype(jnp.int32), axis=1)
    steps = jnp.arange(length, dtype=jnp.int32)
    line = ((target * length * capacity + rank)[:, None] + steps[None, :] * capacity).reshape(-1)
    dispatch = (
        jnp.arange(paths * length * capacity, dtype=jnp.int32)[:, None] == line[None, :]
    ).astype(jnp.bfloat16)
    outgoing = jnp.dot(
        dispatch, docs.reshape(count * length, width), preferred_element_type=jnp.float32
    ).astype(jnp.bfloat16)
    tally = jnp.sum(
        (target[None, :] == jnp.arange(paths, dtype=jnp.int32)[:, None]).astype(jnp.float32), axis=1
    )
    tallies = jnp.broadcast_to(tally[:, None, None], (paths, 8, 128))
    arrived, counts, whole_one, whole_two = exchange(
        n_row,
        n_col,
        outgoing.reshape(paths, length * capacity, width),
        tallies,
        level_one[0].astype(jnp.bfloat16),
        level_two[0].astype(jnp.bfloat16),
    )
    total = jnp.sum(counts[:, 0, 0]) * (length - 1)
    blocks = arrived.astype(jnp.float32)
    inputs = blocks[:, : (length - 1) * capacity].reshape(-1, width)
    targets = blocks[:, capacity:].reshape(-1, width)
    whole_one = whole_one.reshape(width, width).astype(jnp.float32)
    whole_two = whole_two.reshape(width, width).astype(jnp.float32)
    end_one, end_two = train_path(whole_one, whole_two, inputs, targets, total)
    share_one, share_two = scatter(
        n_row,
        n_col,
        (whole_one - end_one).astype(jnp.bfloat16),
        (whole_two - end_two).astype(jnp.bfloat16),
    )
    delta_one = (share_one / n_col)[None]
    delta_two = (share_two / n_row)[None]
    next_moment_one = momentum_decay * moment_one + delta_one
    next_moment_two = momentum_decay * moment_two + delta_two
    new_one = level_one - outer_rate * (delta_one + momentum_decay * next_moment_one)
    new_two = level_two - outer_rate * (delta_two + momentum_decay * next_moment_two)
    return (new_one, new_two, next_moment_one, next_moment_two)


def solution(mesh):
    placed = (
        P(("row", "col"), None, None),
        P(("row", "col"), None),
        P("row", "col", None),
        P("col", "row", None),
        P("row", "col", None),
        P("col", "row", None),
    )
    return jax.shard_map(
        shards,
        mesh=mesh,
        in_specs=placed,
        out_specs=(
            P("row", "col", None),
            P("col", "row", None),
            P("row", "col", None),
            P("col", "row", None),
        ),
        check_vma=False,
    )
```

profile of v0, /device:TPU:0, one launch (start us, length us, event | category | flops | bytes accessed | tf_op | source)
XLA Modules:
  0.0 150.5 jit_solution(18241190857139960985)
XLA Ops:
  0.6 0.9 convert_reduce_fusion
  1.5 0.7 fusion.126
  2.2 0.8 convert_reduce_fusion.1
  3.0 0.1 broadcast_add_fusion
  3.1 0.1 add.113
  3.2 0.8 broadcast_in_dim.14.cnt_ref
  3.9 1.7 %convert_bitcast_fusion.1.one_ref = bf16[112,896]{1,0:T(8,128)(2,1)} fusion(f32[1,112,896]{2,1,0:T(8,128)} %param.8), kind=kLoop, calls=%fused_computation.135 | loop fusion | flops 100352 | bytes 602112 | tf_op jit(solution)/shard_map/convert_element_type | solution.py:384
  5.6 1.9 %convert_bitcast_fusion.two_ref = bf16[224,896]{1,0:T(8,128)(2,1)} fusion(f32[1,224,896]{2,1,0:T(8,128)} %param.9), kind=kLoop, calls=%fused_computation.134 | loop fusion | flops 200704 | bytes 1204224 | tf_op jit(solution)/shard_map/convert_element_type | solution.py:385
  7.6 1.6 %reshape.127 = bf16[512,896]{1,0:T(8,128)(2,1)S(1)} reshape(bf16[128,4,896]{2,1,0:T(4,128)(2,1)} %param.6) | data formatting | bytes 1835008 | tf_op jit(solution)/shard_map/reshape | solution.py:373
  9.2 2.5 %fusion.59 = bf16[1024,896]{1,0:T(8,128)(2,1)} fusion(bf16[512,896]{1,0:T(8,128)(2,1)S(1)} %reshape.127, s32[512]{0:T(512)S(1)} %add.113), kind=kOutput, calls=%fused_computation.93 | convolution fusion | flops 940965888 | bytes 2754560 | tf_op jit(solution)/shard_map/dot_general | solution.py:372
  11.7 63.8 %shard_map.93 = (bf16[32,32,896]{2,1,0:T(8,128)(2,1)}, f32[32,8,128]{2,1,0:T(8,128)}, bf16[8,112,896]{2,1,0:T(8,128)(2,1)}, bf16[4,224,896]{2,1,0:T(8,128)(2,1)}) custom-call(bf16[32,32,896]{2,1,0:T(8,128)(2,1)} %bitcast.77, f32[32,8,128]{2,1,0:T(8,128)} %broadcast_in_dim.14.cnt_ref, bf16[112,896]{1,0:T(8,128)(2,1)} %convert_bitcast_fusion.1.one_ref, ...), custom_call_target="tpu_custom_call" | custom-call | tf_op jit(solution)/shard_map/pallas_call | solution.py:224
  75.5 1.5 %slice_reduce_fusion = f32[]{:T(128)} fusion(f32[32,8,128]{2,1,0:T(8,128)} %get-tuple-element.13), kind=kLoop, calls=%fused_computation.140 | loop fusion | flops 31 | bytes 132 | tf_op jit(solution)/shard_map/reduce_sum | solution.py:387
  77.7 2.0 %convert_element_type.130 = f32[32,32,896]{2,1,0:T(8,128)S(1)} convert(bf16[32,32,896]{2,1,0:T(8,128)(2,1)} %get-tuple-element.11) | non-fusion elementwise | flops 917504 | bytes 5505024 | tf_op jit(solution)/shard_map/convert_element_type | solution.py:388
  79.7 0.2 multiply_reduce_fusion.3
  80.0 0.0 copy-start
  80.0 0.2 multiply_convert_fusion.3
  80.2 0.1 rsqrt.45
  80.3 1.2 copy-done
  81.5 0.0 copy-start.6
  81.5 0.4 fusion.143
  81.8 1.1 copy-done.6
  82.9 0.0 copy-start.1
  82.9 2.4 %multiply_reduce_fusion.2 = (f32[768]{0:T(1024)S(1)}, f32[768,896]{1,0:T(8,128)S(1)}, bf16[768,896]{1,0:T(8,128)(2,1)S(1)}, f32[768,896]{1,0:T(8,128)S(1)}) fusion(f32[32,24,896]{2,1,0:T(8,128)S(1)} %get-tuple-element.28, f32[768]{0:T(1024)S(1)} %rsqrt.45, bf16[768,896]{1,0:T(8,128)(2,1)S(1)} %bitcast.80, bf16[896,896]{1,0:T(8,128)(2,1)S(1)} %bitcast.81), kind=kOutput, calls=%fused_computation.70 | convolution fusion | flops 1240005888 | bytes 12621824 | tf_op jit(solution)/shard_map/jvp()/dot_general | solution.py:28
  85.3 0.0 copy-done.1
  85.3 1.8 %fusion.26 = f32[768,896]{1,0:T(8,128)S(1)} fusion(f32[32,24,896]{2,1,0:T(8,128)S(1)} %get-tuple-element.27, f32[768,896]{1,0:T(8,128)S(1)} %get-tuple-element.25, bf16[896,896]{1,0:T(8,128)(2,1)S(1)} %bitcast.72, f32[]{:T(128)S(6)} %mul.315, f32[768]{0:T(1024)S(1)} %fusion.123), kind=kOutput, calls=%fused_computation.44 | convolution fusion | flops 1237942272 | bytes 9866244 | tf_op jit(solution)/shard_map/jvp()/dot_general | solution.py:38
  87.1 1.8 %fusion.5 = (f32[768]{0:T(1024)S(1)}, bf16[768,896]{1,0:T(8,128)(2,1)S(1)}) fusion(f32[768,896]{1,0:T(8,128)S(1)} %get-tuple-element.25, bf16[896,896]{1,0:T(8,128)(2,1)S(1)} %bitcast.73, f32[768,896]{1,0:T(8,128)S(1)} %fusion.26), kind=kOutput, calls=%fused_computation.23 | convolution fusion | flops 1236565248 | bytes 8489984 | tf_op jit(solution)/shard_map/transpose(jvp())/dot_general | solution.py:38
  89.0 2.7 %fusion.75 = bf16[896,896]{1,0:T(8,128)(2,1)S(1)} fusion(bf16[768,896]{1,0:T(8,128)(2,1)S(1)} %get-tuple-element.26, f32[768,896]{1,0:T(8,128)S(1)} %fusion.26, bf16[768,896]{1,0:T(8,128)(2,1)S(1)} %get-tuple-element.31, f32[768,896]{1,0:T(8,128)S(1)} %get-tuple-element.25, f32[768,896]{1,0:T(8,128)S(1)} %get-tuple-element.29, ...), kind=kOutput, calls=%fused_computation.99 | convolution fusion | flops 1245626368 | bytes 12621824 | tf_op jit(solution)/shard_map/transpose(jvp())/dot_general | solution.py:28
  91.7 1.7 %fusion.60 = bf16[896,896]{1,0:T(8,128)(2,1)S(1)} fusion(f32[768,896]{1,0:T(8,128)S(1)} %fusion.26, f32[768,896]{1,0:T(8,128)S(1)} %get-tuple-element.25, f32[768]{0:T(1024)S(1)} %fusion.123), kind=kOutput, calls=%fused_computation.94 | convolution fusion | flops 1235992576 | bytes 7113728 | tf_op jit(solution)/shard_map/transpose(jvp())/dot_general | solution.py:38
  93.4 2.5 %multiply_reduce_fusion.1 = (f32[768]{0:T(1024)S(1)}, f32[768,896]{1,0:T(8,128)S(1)}, f32[768,896]{1,0:T(8,128)S(1)}) fusion(f32[32,24,896]{2,1,0:T(8,128)S(1)} %get-tuple-element.28, bf16[768,896]{1,0:T(8,128)(2,1)S(1)} %get-tuple-element.26, bf16[896,896]{1,0:T(8,128)(2,1)S(1)} %fusion.75, bf16[896,896]{1,0:T(8,128)(2,1)S(1)} %bitcast.82), kind=kOutput, calls=%fused_computation.64 | convolution fusion | flops 1242643712 | bytes 12848128 | tf_op jit(solution)/shard_map/jvp()/dot_general | solution.py:28
  96.0 1.9 %fusion.28 = f32[768,896]{1,0:T(8,128)S(1)} fusion(f32[32,24,896]{2,1,0:T(8,128)S(1)} %get-tuple-element.27, f32[768,896]{1,0:T(8,128)S(1)} %get-tuple-element.23, f32[]{:T(128)S(6)} %mul.315, f32[768]{0:T(1024)S(1)} %fusion.124, bf16[896,896]{1,0:T(8,128)(2,1)S(1)} %fusion.60, bf16[896,896]{1,0:T(8,128)(2,1)S(1)} %bitcast.74), kind=kOutput, calls=%fused_computation.46 | convolution fusion | flops 1241956352 | bytes 11471876 | tf_op jit(solution)/shard_map/jvp()/dot_general | solution.py:38
  97.9 1.9 %fusion.7 = (f32[768]{0:T(1024)S(1)}, bf16[768,896]{1,0:T(8,128)(2,1)S(1)}) fusion(f32[768,896]{1,0:T(8,128)S(1)} %get-tuple-element.23, bf16[896,896]{1,0:T(8,128)(2,1)S(1)} %fusion.60, bf16[896,896]{1,0:T(8,128)(2,1)S(1)} %bitcast.75, f32[768,896]{1,0:T(8,128)S(1)} %fusion.28), kind=kOutput, calls=%fused_computation.25 | convolution fusion | flops 1240579328 | bytes 10095616 | tf_op jit(solution)/shard_map/transpose(jvp())/dot_general | solution.py:38
  99.8 2.8 %fusion.72 = bf16[896,896]{1,0:T(8,128)(2,1)S(1)} fusion(bf16[768,896]{1,0:T(8,128)(2,1)S(1)} %get-tuple-element.26, f32[768,896]{1,0:T(8,128)S(1)} %fusion.28, bf16[768,896]{1,0:T(8,128)(2,1)S(1)} %get-tuple-element.34, f32[768,896]{1,0:T(8,128)S(1)} %get-tuple-element.23, f32[768,896]{1,0:T(8,128)S(1)} %get-tuple-element.32, ...), kind=kOutput, calls=%fused_computation.98 | convolution fusion | flops 1245626368 | bytes 12621824 | tf_op jit(solution)/shard_map/transpose(jvp())/dot_general | solution.py:28
  102.6 2.1 %fusion.57 = (bf16[896,896]{1,0:T(8,128)(2,1)S(1)}, bf16[896,896]{1,0:T(8,128)(2,1)S(1)}) fusion(bf16[896,896]{1,0:T(8,128)(2,1)S(1)} %fusion.60, bf16[4,224,896]{2,1,0:T(8,128)(2,1)S(1)} %copy-done.1, f32[768,896]{1,0:T(8,128)S(1)} %fusion.28, f32[768,896]{1,0:T(8,128)S(1)} %get-tuple-element.23, f32[768]{0:T(1024)S(1)} %fusion.124), kind=kOutput, calls=%fused_computation.90 | convolution fusion | flops 1242415104 | bytes 11930624 | tf_op jit(solution)/shard_map/transpose(jvp())/dot_general | solution.py:38
  104.7 2.4 %multiply_reduce_fusion = (f32[768]{0:T(1024)S(1)}, f32[768,896]{1,0:T(8,128)S(1)}, f32[768,896]{1,0:T(8,128)S(1)}) fusion(f32[32,24,896]{2,1,0:T(8,128)S(1)} %get-tuple-element.28, bf16[768,896]{1,0:T(8,128)(2,1)S(1)} %get-tuple-element.26, bf16[896,896]{1,0:T(8,128)(2,1)S(1)} %fusion.72, bf16[896,896]{1,0:T(8,128)(2,1)S(1)} %fusion.75, ...), kind=kOutput, calls=%fused_computation.58 | convolution fusion | flops 1245052160 | bytes 14453760 | tf_op jit(solution)/shard_map/jvp()/dot_general | solution.py:28
  107.1 2.1 %fusion.30 = f32[768,896]{1,0:T(8,128)S(1)} fusion(f32[32,24,896]{2,1,0:T(8,128)S(1)} %get-tuple-element.27, f32[768,896]{1,0:T(8,128)S(1)} %get-tuple-element.21, bf16[896,896]{1,0:T(8,128)(2,1)S(1)} %get-tuple-element.36, f32[]{:T(128)S(6)} %mul.315, f32[768]{0:T(1024)S(1)} %fusion.125), kind=kOutput, calls=%fused_computation.48 | convolution fusion | flops 1237942272 | bytes 9866244 | tf_op jit(solution)/shard_map/jvp()/dot_general | solution.py:38
  109.2 3.6 %fusion.1 = bf16[896,896]{1,0:T(8,128)(2,1)} fusion(bf16[896,896]{1,0:T(8,128)(2,1)S(1)} %bitcast.76, bf16[896,896]{1,0:T(8,128)(2,1)S(1)} %get-tuple-element.37, bf16[896,896]{1,0:T(8,128)(2,1)S(1)} %fusion.60, f32[768,896]{1,0:T(8,128)S(1)} %fusion.30, f32[768,896]{1,0:T(8,128)S(1)} %get-tuple-element.21, f32[768]{0:T(1024)S(1)} %fusion.125), kind=kOutput, calls=%fused_computation.17 | convolution fusion | flops 1245626368 | bytes 11930624 | tf_op jit(solution)/shard_map/transpose(jvp())/dot_general | solution.py:38
  112.8 1.8 %fusion.9 = (f32[768]{0:T(1024)S(1)}, bf16[768,896]{1,0:T(8,128)(2,1)S(1)}) fusion(f32[768,896]{1,0:T(8,128)S(1)} %get-tuple-element.21, bf16[896,896]{1,0:T(8,128)(2,1)S(1)} %get-tuple-element.36, f32[768,896]{1,0:T(8,128)S(1)} %fusion.30), kind=kOutput, calls=%fused_computation.27 | convolution fusion | flops 1236565248 | bytes 8489984 | tf_op jit(solution)/shard_map/transpose(jvp())/dot_general | solution.py:38
  114.6 4.6 %fusion = bf16[896,896]{1,0:T(8,128)(2,1)} fusion(bf16[896,896]{1,0:T(8,128)(2,1)S(1)} %bitcast.84, bf16[896,896]{1,0:T(8,128)(2,1)S(1)} %fusion.72, bf16[896,896]{1,0:T(8,128)(2,1)S(1)} %fusion.75, bf16[768,896]{1,0:T(8,128)(2,1)S(1)} %get-tuple-element.26, f32[768,896]{1,0:T(8,128)S(1)} %fusion.30, bf16[768,896]{1,0:T(8,128)(2,1)S(1)} %get-tuple-element.39, ...), kind=kOutput, calls=%fused_computation.16 | convolution fusion | flops 1255260160 | bytes 17438720 | tf_op jit(solution)/shard_map/transpose(jvp())/dot_general | solution.py:28
  119.2 0.0 copy-start.3
  119.2 0.0 copy-start.5
  119.2 0.0 copy-start.2
  119.2 26.8 %shard_map.94 = (f32[112,896]{1,0:T(8,128)}, f32[224,896]{1,0:T(8,128)}) custom-call(bf16[8,112,896]{2,1,0:T(8,128)(2,1)} %bitcast.79, bf16[4,224,896]{2,1,0:T(8,128)(2,1)} %bitcast.78), custom_call_target="tpu_custom_call" | custom-call | tf_op jit(solution)/shard_map/pallas_call | solution.py:332
  146.0 0.0 copy-done.3
  146.0 0.0 copy-done.5
  146.0 2.0 %fusion.121 = (f32[1,112,896]{2,1,0:T(8,128)}, f32[1,112,896]{2,1,0:T(8,128)}) fusion(f32[1,112,896]{2,1,0:T(8,128)S(1)} %copy-done.3, f32[112,896]{1,0:T(8,128)} %get-tuple-element.14, f32[1,112,896]{2,1,0:T(8,128)S(1)} %copy-done.5), kind=kLoop, calls=%fused_computation.133 | loop fusion | flops 702464 | bytes 2007040 | tf_op jit(solution)/shard_map/sub | solution.py:404
  148.0 0.0 copy-done.2
  148.0 0.0 copy-done.4
  148.0 2.5 %fusion.117 = (f32[1,224,896]{2,1,0:T(8,128)}, f32[1,224,896]{2,1,0:T(8,128)}) fusion(f32[1,224,896]{2,1,0:T(8,128)S(1)} %copy-done.2, f32[224,896]{1,0:T(8,128)} %get-tuple-element.15, f32[1,224,896]{2,1,0:T(8,128)S(1)} %copy-done.4), kind=kLoop, calls=%fused_computation.129 | loop fusion | flops 1404928 | bytes 4014080 | tf_op jit(solution)/shard_map/sub | solution.py:405
  (9 shorter events, 0.1 us)
Async XLA Ops:
  80.0 1.5 copy-start
  81.5 1.4 copy-start.6
  82.9 2.4 %copy-start.1 = (bf16[4,224,896]{2,1,0:T(8,128)(2,1)S(1)}, bf16[4,224,896]{2,1,0:T(8,128)(2,1)}, u32[]{:S(2)}) copy-start(bf16[4,224,896]{2,1,0:T(8,128)(2,1)} %get-tuple-element.12) | copy-start | bytes 4816900
  119.2 26.8 %copy-start.3 = (f32[1,112,896]{2,1,0:T(8,128)S(1)}, f32[1,112,896]{2,1,0:T(8,128)}, u32[]{:S(2)}) copy-start(f32[1,112,896]{2,1,0:T(8,128)} %param.8) | copy-start | bytes 1204228
  119.2 26.8 %copy-start.5 = (f32[1,112,896]{2,1,0:T(8,128)S(1)}, f32[1,112,896]{2,1,0:T(8,128)}, u32[]{:S(2)}) copy-start(f32[1,112,896]{2,1,0:T(8,128)} %param.10) | copy-start | bytes 1204228
  119.2 28.8 %copy-start.2 = (f32[1,224,896]{2,1,0:T(8,128)S(1)}, f32[1,224,896]{2,1,0:T(8,128)}, u32[]{:S(2)}) copy-start(f32[1,224,896]{2,1,0:T(8,128)} %param.9) | copy-start | bytes 2408452
  119.2 28.8 %copy-start.4 = (f32[1,224,896]{2,1,0:T(8,128)S(1)}, f32[1,224,896]{2,1,0:T(8,128)}, u32[]{:S(2)}) copy-start(f32[1,224,896]{2,1,0:T(8,128)} %param.11) | copy-start | bytes 2408452
where the time goes:
time: 151 us
  Pallas kernels  90.5 us (60%)
  matrix products  38.7 us (26%)
  other arithmetic  14.6 us (10%)
  local copies, waits for them, and re-layouts  5.17 us (3%)
  between operations  1.53 us (1%)
    pallas_call x1, Pallas kernels, exchange(): pl.pallas_call(functools.partial(exchange_kernel, n_row, n_col), out_shap...  63.8 us
    pallas_call x1, Pallas kernels, scatter(): pl.pallas_call(functools.partial(scatter_kernel, n_row, n_col), out_shape...  26.8 us
    dot_general x9, matrix products, path_loss(): jnp.dot(normalize(hidden).astype(jnp.bfloat16), second.astype(jnp.bfloat1...  18.8 us
    dot_general x6, matrix products, path_loss(): jnp.dot(normalize(inputs).astype(jnp.bfloat16), first.astype(jnp.bfloat16...  17.4 us

commit v1 on v0

--- a/solution.py
+++ b/solution.py
@@ -55,8 +55,9 @@
 
 
 def exchange_kernel(
-    n_row, n_col, out_ref, cnt_ref, one_ref, two_ref,
+    n_row, n_col, line_ref, docs_ref, level_one_ref, level_two_ref,
     arrived, counts, whole_one, whole_two,
+    out_ref, cnt_ref, one_ref, two_ref,
     doc_send, doc_recv, cnt_send, cnt_recv, up_send, down_send, one_recv,
     pair_send, pair_recv, two_send, two_recv, local_sem,
 ):
@@ -65,27 +66,20 @@
     me = row * n_col + col
     chips = n_col // 2
     place, core = col // 2, col % 2
-
-    def device(index):
-        return {"row": index // n_col, "col": index % n_col}
-
+    lines, width = arrived.shape[1:]
+    depth = docs_ref.shape[0]
     barrier = pltpu.get_barrier_semaphore()
 
     def greet(k, carry):
+        to = (me + k) % n
         pl.semaphore_signal(
-            barrier, inc=1, device_id=device((me + k) % n), device_id_type=MESH
+            barrier, inc=1, device_id={"row": to // n_col, "col": to % n_col}, device_id_type=MESH
         )
         return carry
 
     lax.fori_loop(1, n, greet, 0)
-    own = [
-        pltpu.make_async_copy(out_ref.at[me], arrived.at[me], local_sem.at[0]),
-        pltpu.make_async_copy(cnt_ref.at[me], counts.at[me], local_sem.at[1]),
-        pltpu.make_async_copy(one_ref, whole_one.at[col], local_sem.at[2]),
-        pltpu.make_async_copy(two_ref, whole_two.at[row], local_sem.at[3]),
-    ]
-    for copy in own:
-        copy.start()
+    one_ref[...] = level_one_ref[...].astype(jnp.bfloat16)
+    two_ref[...] = level_two_ref[...].astype(jnp.bfloat16)
     pl.semaphore_wait(barrier, n - 1)
 
     def along(source, block, to, send):
@@ -129,63 +123,90 @@
             device_id_type=MESH,
         )
 
-    def doc_copy(k):
-        to = (me + k) % n
-        return pltpu.make_async_remote_copy(
-            src_ref=out_ref.at[to],
-            dst_ref=arrived.at[me],
-            send_sem=doc_send.at[k],
-            recv_sem=doc_recv.at[k],
-            device_id=device(to),
-            device_id_type=MESH,
-        )
-
-    def cnt_copy(k):
-        to = (me + k) % n
-        return pltpu.make_async_remote_copy(
-            src_ref=cnt_ref.at[to],
-            dst_ref=counts.at[me],
-            send_sem=cnt_send.at[k],
-            recv_sem=cnt_recv.at[k],
-            device_id=device(to),
-            device_id_type=MESH,
-        )
-
-    def send_docs(low, high):
-        def body(k, carry):
-            doc_copy(k).start()
-            cnt_copy(k).start()
+    for k in range(1, n_row):
+        two_copy(k).start()
+
+    own = [
+        pltpu.make_async_copy(one_ref, whole_one.at[col], local_sem.at[0]),
+        pltpu.make_async_copy(two_ref, whole_two.at[row], local_sem.at[1]),
+        pltpu.make_async_copy(out_ref.at[me], arrived.at[me], local_sem.at[2]),
+        pltpu.make_async_copy(cnt_ref.at[me], counts.at[me], local_sem.at[3]),
+    ]
+    own[0].start()
+    own[1].start()
+
+    path = lax.broadcasted_iota(jnp.int32, (n, 8, depth), 0) * lines
+    wide = jnp.broadcast_to(line_ref[...][None], (n, 8, depth))
+    named = ((wide >= path) & (wide < path + lines)).astype(jnp.float32)
+    cnt_ref[...] = jnp.broadcast_to(jnp.sum(named, axis=-1, keepdims=True), cnt_ref.shape)
+
+    def pair_of(shift, turn):
+        to_row, to_col = (row + shift) % n_row, (col + turn) % n_col
+        to = to_row * n_col + to_col
+        k = shift * n_col + turn
+        peer = {"row": to_row, "col": to_col}
+        return (
+            pltpu.make_async_remote_copy(
+                src_ref=out_ref.at[to],
+                dst_ref=arrived.at[me],
+                send_sem=doc_send.at[k],
+                recv_sem=doc_recv.at[k],
+                device_id=peer,
+                device_id_type=MESH,
+            ),
+            pltpu.make_async_remote_copy(
+                src_ref=cnt_ref.at[to],
+                dst_ref=counts.at[me],
+                send_sem=cnt_send.at[k],
+                recv_sem=cnt_recv.at[k],
+                device_id=peer,
+                device_id_type=MESH,
+            ),
+        )
+
+    def send_group(shift):
+        to_row = (row + shift) % n_row
+        base = to_row * n_col * lines
+        index = lax.broadcasted_iota(jnp.int32, (n_col * lines, depth), 0) + base
+        dispatch = (index == line_ref[...]).astype(jnp.float32).astype(jnp.bfloat16)
+        rows = jnp.dot(dispatch, docs_ref[...], preferred_element_type=jnp.float32)
+        out_ref[pl.ds(to_row * n_col, n_col)] = rows.reshape(n_col, lines, width).astype(
+            jnp.bfloat16
+        )
+
+        def body(turn, carry):
+            for copy in pair_of(shift, turn):
+                copy.start()
             return carry
 
-        lax.fori_loop(low, high, body, 0)
-
-    def send_two(k, carry):
-        two_copy(k).start()
-        return carry
-
-    lax.fori_loop(1, n_row, send_two, 0)
-    cuts = [1 + (n - 1) * i // (chips - 1) for i in range(chips)]
-    for step in range(1, chips):
-        send_docs(cuts[step - 1], cuts[step])
-        low, high = col - 2 * step, col + 2 * step
-
-        @pl.when(place >= step)
-        def _():
-            along(one_ref, low, col, up_send).wait_recv()
-            across(whole_one.at[low], low).start()
-
-        @pl.when((place >= step) & (place < chips - 1))
-        def _():
-            along(whole_one.at[low], low, col + 2, up_send).start()
-
-        @pl.when(place < chips - step)
-        def _():
-            along(one_ref, high, col, down_send).wait_recv()
-            across(whole_one.at[high], high).start()
-
-        @pl.when((place < chips - step) & (place > 0))
-        def _():
-            along(whole_one.at[high], high, col - 2, down_send).start()
+        lax.fori_loop(1 if shift == 0 else 0, n_col, body, 0)
+        if shift == 0:
+            own[2].start()
+            own[3].start()
+
+    for step in range(1, max(n_row, chips - 1) + 1):
+        if step <= n_row:
+            send_group(step % n_row)
+        if step < chips:
+            low, high = col - 2 * step, col + 2 * step
+
+            @pl.when(place >= step)
+            def _():
+                along(one_ref, low, col, up_send).wait_recv()
+                across(whole_one.at[low], low).start()
+
+            @pl.when((place >= step) & (place < chips - 1))
+            def _():
+                along(whole_one.at[low], low, col + 2, up_send).start()
+
+            @pl.when(place < chips - step)
+            def _():
+                along(one_ref, high, col, down_send).wait_recv()
+                across(whole_one.at[high], high).start()
+
+            @pl.when((place < chips - step) & (place > 0))
+            def _():
+                along(whole_one.at[high], high, col - 2, down_send).start()
 
     for copy in own:
         copy.wait()
@@ -203,41 +224,45 @@
         def _():
             along(one_ref, block, col - 2, down_send).wait_send()
 
-    def end_two(k, carry):
+    for k in range(1, n_row):
         two_copy(k).wait()
-        return carry
-
-    lax.fori_loop(1, n_row, end_two, 0)
-
-    def end_docs(k, carry):
-        doc_copy(k).wait()
-        cnt_copy(k).wait()
-        return carry
-
-    lax.fori_loop(1, n, end_docs, 0)
-
-
-def exchange(n_row, n_col, outgoing, tallies, level_one, level_two):
+
+    for shift in range(n_row):
+
+        def finish(turn, carry):
+            for copy in pair_of(shift, turn):
+                copy.wait()
+            return carry
+
+        lax.fori_loop(1 if shift == 0 else 0, n_col, finish, 0)
+
+
+def exchange(n_row, n_col, lines, line, docs, level_one, level_two):
     n = n_row * n_col
+    width = docs.shape[-1]
     vmem = pl.BlockSpec(memory_space=pltpu.VMEM)
     dma = pltpu.SemaphoreType.DMA
     return pl.pallas_call(
         functools.partial(exchange_kernel, n_row, n_col),
         out_shape=(
-            jax.ShapeDtypeStruct(outgoing.shape, outgoing.dtype),
-            jax.ShapeDtypeStruct(tallies.shape, tallies.dtype),
-            jax.ShapeDtypeStruct((n_col,) + level_one.shape, level_one.dtype),
-            jax.ShapeDtypeStruct((n_row,) + level_two.shape, level_two.dtype),
+            jax.ShapeDtypeStruct((n, lines, width), jnp.bfloat16),
+            jax.ShapeDtypeStruct((n, 8, 128), jnp.float32),
+            jax.ShapeDtypeStruct((n_col,) + level_one.shape, jnp.bfloat16),
+            jax.ShapeDtypeStruct((n_row,) + level_two.shape, jnp.bfloat16),
         ),
         in_specs=[vmem] * 4,
         out_specs=(vmem,) * 4,
         scratch_shapes=[
+            pltpu.VMEM((n, lines, width), jnp.bfloat16),
+            pltpu.VMEM((n, 8, 128), jnp.float32),
+            pltpu.VMEM(level_one.shape, jnp.bfloat16),
+            pltpu.VMEM(level_two.shape, jnp.bfloat16),
             dma((n,)), dma((n,)), dma((n,)), dma((n,)),
             dma((n_col,)), dma((n_col,)), dma((n_col,)), dma((n_col,)), dma((n_col,)),
             dma((n_row,)), dma((n_row,)), dma((4,)),
         ],
         compiler_params=pltpu.CompilerParams(collective_id=0, has_side_effects=True),
-    )(outgoing, tallies, level_one, level_two)
+    )(line, docs, level_one, level_two)
 
 
 def scatter_kernel(
@@ -366,25 +391,16 @@
     rank = jnp.sum(same.astype(jnp.int32), axis=1)
     steps = jnp.arange(length, dtype=jnp.int32)
     line = ((target * length * capacity + rank)[:, None] + steps[None, :] * capacity).reshape(-1)
-    dispatch = (
-        jnp.arange(paths * length * capacity, dtype=jnp.int32)[:, None] == line[None, :]
-    ).astype(jnp.bfloat16)
-    outgoing = jnp.dot(
-        dispatch, docs.reshape(count * length, width), preferred_element_type=jnp.float32
-    ).astype(jnp.bfloat16)
-    tally = jnp.sum(
-        (target[None, :] == jnp.arange(paths, dtype=jnp.int32)[:, None]).astype(jnp.float32), axis=1
-    )
-    tallies = jnp.broadcast_to(tally[:, None, None], (paths, 8, 128))
     arrived, counts, whole_one, whole_two = exchange(
         n_row,
         n_col,
-        outgoing.reshape(paths, length * capacity, width),
-        tallies,
-        level_one[0].astype(jnp.bfloat16),
-        level_two[0].astype(jnp.bfloat16),
-    )
-    total = jnp.sum(counts[:, 0, 0]) * (length - 1)
+        length * capacity,
+        line[None, :],
+        docs.reshape(count * length, width),
+        level_one[0],
+        level_two[0],
+    )
+    total = jnp.sum(counts[:, 0, 0]) * ((length - 1) / length)
     blocks = arrived.astype(jnp.float32)
     inputs = blocks[:, : (length - 1) * capacity].reshape(-1, width)
     targets = blocks[:, capacity:].reshape(-1, width)

time: 151 us -> 144 us (0.954)
  other arithmetic: 14.6 us -> 10.2 us
  matrix products: 38.7 us -> 36.2 us
    convert_element_type x2 -> x0, other arithmetic: 3.63 us -> none  [the longest x1 1.93 us: shards(): level_two[0].astype(jnp.bfloat16)]
    dot_general x1 -> x0, matrix products: 2.5 us -> none  [shards(): jnp.dot(dispatch, docs.reshape(count * length, width), preferred_element_...]
where the time goes in v1:
time: 144 us
  Pallas kernels  90.3 us (63%)
  matrix products  36.2 us (25%)
  other arithmetic  10.2 us (7%)
  local copies, waits for them, and re-layouts  5.76 us (4%)
  between operations  1.51 us (1%)
    pallas_call x1, Pallas kernels, exchange(): pl.pallas_call(functools.partial(exchange_kernel, n_row, n_col), out_shap...  62.8 us
    pallas_call x1, Pallas kernels, scatter(): pl.pallas_call(functools.partial(scatter_kernel, n_row, n_col), out_shape...  27.4 us
    dot_general x9, matrix products, path_loss(): jnp.dot(normalize(hidden).astype(jnp.bfloat16), second.astype(jnp.bfloat1...  18.8 us
    dot_general x6, matrix products, path_loss(): jnp.dot(normalize(inputs).astype(jnp.bfloat16), first.astype(jnp.bfloat16...  17.4 us

profile of v1, /device:TPU:0, one launch (start us, length us, event | category | flops | bytes accessed | tf_op | source)
XLA Modules:
  0.0 143.9 jit_solution(7254087877503624157)
XLA Ops:
  0.6 0.9 convert_reduce_fusion
  1.5 0.7 fusion.123
  2.2 0.1 broadcast_add_fusion
  2.3 0.7 add.116.line_ref
  3.0 2.4 %reshape.129.docs_ref = bf16[512,896]{1,0:T(8,128)(2,1)} reshape(bf16[128,4,896]{2,1,0:T(4,128)(2,1)} %param.6) | data formatting | bytes 1835008 | tf_op jit(solution)/shard_map/reshape | solution.py:399
  5.4 62.8 %shard_map.93 = (bf16[32,32,896]{2,1,0:T(8,128)(2,1)}, f32[32,8,128]{2,1,0:T(8,128)}, bf16[8,112,896]{2,1,0:T(8,128)(2,1)}, bf16[4,224,896]{2,1,0:T(8,128)(2,1)}) custom-call(s32[1,512]{1,0:T(1,128)} %add.116.line_ref, bf16[512,896]{1,0:T(8,128)(2,1)} %reshape.129.docs_ref, f32[112,896]{1,0:T(8,128)} %bitcast.76, f32[224,896]{1,0:T(8,128)} %bitcast.73), custom_call_target="tpu_custom_call" | custom-call | tf_op jit(solution)/shard_map/pallas_call | solution.py:245
  68.2 1.5 %slice_reduce_fusion = f32[]{:T(128)} fusion(f32[32,8,128]{2,1,0:T(8,128)} %get-tuple-element.13), kind=kLoop, calls=%fused_computation.134 | loop fusion | flops 31 | bytes 132 | tf_op jit(solution)/shard_map/reduce_sum | solution.py:403
  70.5 2.0 %convert_element_type.107 = f32[32,32,896]{2,1,0:T(8,128)S(1)} convert(bf16[32,32,896]{2,1,0:T(8,128)(2,1)} %get-tuple-element.11) | non-fusion elementwise | flops 917504 | bytes 5505024 | tf_op jit(solution)/shard_map/convert_element_type | solution.py:404
  72.4 0.2 multiply_reduce_fusion.3
  72.7 0.0 copy-start
  72.7 0.2 multiply_convert_fusion.3
  73.0 0.1 rsqrt.45
  73.0 1.2 copy-done
  74.2 0.0 copy-start.6
  74.2 0.4 fusion.140
  74.6 1.1 copy-done.6
  75.6 0.0 copy-start.1
  75.6 2.4 %multiply_reduce_fusion.2 = (f32[768]{0:T(1024)S(1)}, f32[768,896]{1,0:T(8,128)S(1)}, bf16[768,896]{1,0:T(8,128)(2,1)S(1)}, f32[768,896]{1,0:T(8,128)S(1)}) fusion(f32[32,24,896]{2,1,0:T(8,128)S(1)} %get-tuple-element.28, f32[768]{0:T(1024)S(1)} %rsqrt.45, bf16[768,896]{1,0:T(8,128)(2,1)S(1)} %bitcast.77, bf16[896,896]{1,0:T(8,128)(2,1)S(1)} %bitcast.78), kind=kOutput, calls=%fused_computation.70 | convolution fusion | flops 1240005888 | bytes 12621824 | tf_op jit(solution)/shard_map/jvp()/dot_general | solution.py:28
  78.0 0.0 copy-done.1
  78.0 1.8 %fusion.26 = f32[768,896]{1,0:T(8,128)S(1)} fusion(f32[32,24,896]{2,1,0:T(8,128)S(1)} %get-tuple-element.27, f32[768,896]{1,0:T(8,128)S(1)} %get-tuple-element.25, bf16[896,896]{1,0:T(8,128)(2,1)S(1)} %bitcast.68, f32[]{:T(128)S(6)} %mul.315, f32[768]{0:T(1024)S(1)} %fusion.120), kind=kOutput, calls=%fused_computation.44 | convolution fusion | flops 1237942272 | bytes 9866244 | tf_op jit(solution)/shard_map/jvp()/dot_general | solution.py:38
  79.9 1.8 %fusion.5 = (f32[768]{0:T(1024)S(1)}, bf16[768,896]{1,0:T(8,128)(2,1)S(1)}) fusion(f32[768,896]{1,0:T(8,128)S(1)} %get-tuple-element.25, bf16[896,896]{1,0:T(8,128)(2,1)S(1)} %bitcast.69, f32[768,896]{1,0:T(8,128)S(1)} %fusion.26), kind=kOutput, calls=%fused_computation.23 | convolution fusion | flops 1236565248 | bytes 8489984 | tf_op jit(solution)/shard_map/transpose(jvp())/dot_general | solution.py:38
  81.7 2.7 %fusion.73 = bf16[896,896]{1,0:T(8,128)(2,1)S(1)} fusion(bf16[768,896]{1,0:T(8,128)(2,1)S(1)} %get-tuple-element.26, f32[768,896]{1,0:T(8,128)S(1)} %fusion.26, bf16[768,896]{1,0:T(8,128)(2,1)S(1)} %get-tuple-element.31, f32[768,896]{1,0:T(8,128)S(1)} %get-tuple-element.25, f32[768,896]{1,0:T(8,128)S(1)} %get-tuple-element.29, ...), kind=kOutput, calls=%fused_computation.96 | convolution fusion | flops 1245626368 | bytes 12621824 | tf_op jit(solution)/shard_map/transpose(jvp())/dot_general | solution.py:28
  84.4 1.7 %fusion.58 = bf16[896,896]{1,0:T(8,128)(2,1)S(1)} fusion(f32[768,896]{1,0:T(8,128)S(1)} %fusion.26, f32[768,896]{1,0:T(8,128)S(1)} %get-tuple-element.25, f32[768]{0:T(1024)S(1)} %fusion.120), kind=kOutput, calls=%fused_computation.91 | convolution fusion | flops 1235992576 | bytes 7113728 | tf_op jit(solution)/shard_map/transpose(jvp())/dot_general | solution.py:38
  86.2 2.5 %multiply_reduce_fusion.1 = (f32[768]{0:T(1024)S(1)}, f32[768,896]{1,0:T(8,128)S(1)}, f32[768,896]{1,0:T(8,128)S(1)}) fusion(f32[32,24,896]{2,1,0:T(8,128)S(1)} %get-tuple-element.28, bf16[768,896]{1,0:T(8,128)(2,1)S(1)} %get-tuple-element.26, bf16[896,896]{1,0:T(8,128)(2,1)S(1)} %fusion.73, bf16[896,896]{1,0:T(8,128)(2,1)S(1)} %bitcast.79), kind=kOutput, calls=%fused_computation.64 | convolution fusion | flops 1242643712 | bytes 12848128 | tf_op jit(solution)/shard_map/jvp()/dot_general | solution.py:28
  88.7 1.9 %fusion.28 = f32[768,896]{1,0:T(8,128)S(1)} fusion(f32[32,24,896]{2,1,0:T(8,128)S(1)} %get-tuple-element.27, f32[768,896]{1,0:T(8,128)S(1)} %get-tuple-element.23, f32[]{:T(128)S(6)} %mul.315, f32[768]{0:T(1024)S(1)} %fusion.121, bf16[896,896]{1,0:T(8,128)(2,1)S(1)} %fusion.58, bf16[896,896]{1,0:T(8,128)(2,1)S(1)} %bitcast.70), kind=kOutput, calls=%fused_computation.46 | convolution fusion | flops 1241956352 | bytes 11471876 | tf_op jit(solution)/shard_map/jvp()/dot_general | solution.py:38
  90.6 1.9 %fusion.7 = (f32[768]{0:T(1024)S(1)}, bf16[768,896]{1,0:T(8,128)(2,1)S(1)}) fusion(f32[768,896]{1,0:T(8,128)S(1)} %get-tuple-element.23, bf16[896,896]{1,0:T(8,128)(2,1)S(1)} %fusion.58, bf16[896,896]{1,0:T(8,128)(2,1)S(1)} %bitcast.71, f32[768,896]{1,0:T(8,128)S(1)} %fusion.28), kind=kOutput, calls=%fused_computation.25 | convolution fusion | flops 1240579328 | bytes 10095616 | tf_op jit(solution)/shard_map/transpose(jvp())/dot_general | solution.py:38
  92.5 2.8 %fusion.70 = bf16[896,896]{1,0:T(8,128)(2,1)S(1)} fusion(bf16[768,896]{1,0:T(8,128)(2,1)S(1)} %get-tuple-element.26, f32[768,896]{1,0:T(8,128)S(1)} %fusion.28, bf16[768,896]{1,0:T(8,128)(2,1)S(1)} %get-tuple-element.34, f32[768,896]{1,0:T(8,128)S(1)} %get-tuple-element.23, f32[768,896]{1,0:T(8,128)S(1)} %get-tuple-element.32, ...), kind=kOutput, calls=%fused_computation.95 | convolution fusion | flops 1245626368 | bytes 12621824 | tf_op jit(solution)/shard_map/transpose(jvp())/dot_general | solution.py:28
  95.3 2.1 %fusion.57 = (bf16[896,896]{1,0:T(8,128)(2,1)S(1)}, bf16[896,896]{1,0:T(8,128)(2,1)S(1)}) fusion(bf16[896,896]{1,0:T(8,128)(2,1)S(1)} %fusion.58, bf16[4,224,896]{2,1,0:T(8,128)(2,1)S(1)} %copy-done.1, f32[768,896]{1,0:T(8,128)S(1)} %fusion.28, f32[768,896]{1,0:T(8,128)S(1)} %get-tuple-element.23, f32[768]{0:T(1024)S(1)} %fusion.121), kind=kOutput, calls=%fused_computation.90 | convolution fusion | flops 1242415104 | bytes 11930624 | tf_op jit(solution)/shard_map/transpose(jvp())/dot_general | solution.py:38
  97.4 2.4 %multiply_reduce_fusion = (f32[768]{0:T(1024)S(1)}, f32[768,896]{1,0:T(8,128)S(1)}, f32[768,896]{1,0:T(8,128)S(1)}) fusion(f32[32,24,896]{2,1,0:T(8,128)S(1)} %get-tuple-element.28, bf16[768,896]{1,0:T(8,128)(2,1)S(1)} %get-tuple-element.26, bf16[896,896]{1,0:T(8,128)(2,1)S(1)} %fusion.70, bf16[896,896]{1,0:T(8,128)(2,1)S(1)} %fusion.73, ...), kind=kOutput, calls=%fused_computation.58 | convolution fusion | flops 1245052160 | bytes 14453760 | tf_op jit(solution)/shard_map/jvp()/dot_general | solution.py:28
  99.8 2.1 %fusion.30 = f32[768,896]{1,0:T(8,128)S(1)} fusion(f32[32,24,896]{2,1,0:T(8,128)S(1)} %get-tuple-element.27, f32[768,896]{1,0:T(8,128)S(1)} %get-tuple-element.21, bf16[896,896]{1,0:T(8,128)(2,1)S(1)} %get-tuple-element.36, f32[]{:T(128)S(6)} %mul.315, f32[768]{0:T(1024)S(1)} %fusion.122), kind=kOutput, calls=%fused_computation.48 | convolution fusion | flops 1237942272 | bytes 9866244 | tf_op jit(solution)/shard_map/jvp()/dot_general | solution.py:38
  101.9 3.6 %fusion.1 = bf16[896,896]{1,0:T(8,128)(2,1)} fusion(bf16[896,896]{1,0:T(8,128)(2,1)S(1)} %bitcast.72, bf16[896,896]{1,0:T(8,128)(2,1)S(1)} %get-tuple-element.37, bf16[896,896]{1,0:T(8,128)(2,1)S(1)} %fusion.58, f32[768,896]{1,0:T(8,128)S(1)} %fusion.30, f32[768,896]{1,0:T(8,128)S(1)} %get-tuple-element.21, f32[768]{0:T(1024)S(1)} %fusion.122), kind=kOutput, calls=%fused_computation.17 | convolution fusion | flops 1245626368 | bytes 11930624 | tf_op jit(solution)/shard_map/transpose(jvp())/dot_general | solution.py:38
  105.5 1.8 %fusion.9 = (f32[768]{0:T(1024)S(1)}, bf16[768,896]{1,0:T(8,128)(2,1)S(1)}) fusion(f32[768,896]{1,0:T(8,128)S(1)} %get-tuple-element.21, bf16[896,896]{1,0:T(8,128)(2,1)S(1)} %get-tuple-element.36, f32[768,896]{1,0:T(8,128)S(1)} %fusion.30), kind=kOutput, calls=%fused_computation.27 | convolution fusion | flops 1236565248 | bytes 8489984 | tf_op jit(solution)/shard_map/transpose(jvp())/dot_general | solution.py:38
  107.4 4.6 %fusion = bf16[896,896]{1,0:T(8,128)(2,1)} fusion(bf16[896,896]{1,0:T(8,128)(2,1)S(1)} %bitcast.81, bf16[896,896]{1,0:T(8,128)(2,1)S(1)} %fusion.70, bf16[896,896]{1,0:T(8,128)(2,1)S(1)} %fusion.73, bf16[768,896]{1,0:T(8,128)(2,1)S(1)} %get-tuple-element.26, f32[768,896]{1,0:T(8,128)S(1)} %fusion.30, bf16[768,896]{1,0:T(8,128)(2,1)S(1)} %get-tuple-element.39, ...), kind=kOutput, calls=%fused_computation.16 | convolution fusion | flops 1255260160 | bytes 17438720 | tf_op jit(solution)/shard_map/transpose(jvp())/dot_general | solution.py:28
  112.0 0.0 copy-start.3
  112.0 0.0 copy-start.5
  112.0 0.0 copy-start.2
  112.0 0.0 copy-start.4
  112.0 27.4 %shard_map.94 = (f32[112,896]{1,0:T(8,128)}, f32[224,896]{1,0:T(8,128)}) custom-call(bf16[8,112,896]{2,1,0:T(8,128)(2,1)} %bitcast.75, bf16[4,224,896]{2,1,0:T(8,128)(2,1)} %bitcast.74), custom_call_target="tpu_custom_call" | custom-call | tf_op jit(solution)/shard_map/pallas_call | solution.py:357
  139.4 0.0 copy-done.3
  139.4 0.0 copy-done.5
  139.4 2.0 %fusion.118 = (f32[1,112,896]{2,1,0:T(8,128)}, f32[1,112,896]{2,1,0:T(8,128)}) fusion(f32[1,112,896]{2,1,0:T(8,128)S(1)} %copy-done.3, f32[112,896]{1,0:T(8,128)} %get-tuple-element.14, f32[1,112,896]{2,1,0:T(8,128)S(1)} %copy-done.5), kind=kLoop, calls=%fused_computation.129 | loop fusion | flops 702464 | bytes 2007040 | tf_op jit(solution)/shard_map/sub | solution.py:420
  141.4 0.0 copy-done.2
  141.4 0.0 copy-done.4
  141.4 2.5 %fusion.114 = (f32[1,224,896]{2,1,0:T(8,128)}, f32[1,224,896]{2,1,0:T(8,128)}) fusion(f32[1,224,896]{2,1,0:T(8,128)S(1)} %copy-done.2, f32[224,896]{1,0:T(8,128)} %get-tuple-element.15, f32[1,224,896]{2,1,0:T(8,128)S(1)} %copy-done.4), kind=kLoop, calls=%fused_computation.125 | loop fusion | flops 1404928 | bytes 4014080 | tf_op jit(solution)/shard_map/sub | solution.py:421
  (8 shorter events, 0.1 us)
Async XLA Ops:
  72.7 1.5 %copy-start = (bf16[32,32,896]{2,1,0:T(8,128)(2,1)S(1)}, bf16[32,32,896]{2,1,0:T(8,128)(2,1)}, u32[]{:S(2)}) copy-start(bf16[32,32,896]{2,1,0:T(8,128)(2,1)} %get-tuple-element.11) | copy-start | bytes 5505028
  74.2 1.4 copy-start.6
  75.6 2.4 %copy-start.1 = (bf16[4,224,896]{2,1,0:T(8,128)(2,1)S(1)}, bf16[4,224,896]{2,1,0:T(8,128)(2,1)}, u32[]{:S(2)}) copy-start(bf16[4,224,896]{2,1,0:T(8,128)(2,1)} %get-tuple-element.12) | copy-start | bytes 4816900
  112.0 27.5 %copy-start.3 = (f32[1,112,896]{2,1,0:T(8,128)S(1)}, f32[1,112,896]{2,1,0:T(8,128)}, u32[]{:S(2)}) copy-start(f32[1,112,896]{2,1,0:T(8,128)} %param.8) | copy-start | bytes 1204228
  112.0 27.5 %copy-start.5 = (f32[1,112,896]{2,1,0:T(8,128)S(1)}, f32[1,112,896]{2,1,0:T(8,128)}, u32[]{:S(2)}) copy-start(f32[1,112,896]{2,1,0:T(8,128)} %param.10) | copy-start | bytes 1204228
  112.0 29.5 %copy-start.2 = (f32[1,224,896]{2,1,0:T(8,128)S(1)}, f32[1,224,896]{2,1,0:T(8,128)}, u32[]{:S(2)}) copy-start(f32[1,224,896]{2,1,0:T(8,128)} %param.9) | copy-start | bytes 2408452
  112.0 29.5 %copy-start.4 = (f32[1,224,896]{2,1,0:T(8,128)S(1)}, f32[1,224,896]{2,1,0:T(8,128)}, u32[]{:S(2)}) copy-start(f32[1,224,896]{2,1,0:T(8,128)} %param.11) | copy-start | bytes 2408452

commit v2 on v1

--- a/solution.py
+++ b/solution.py
@@ -56,8 +56,8 @@
 
 def exchange_kernel(
     n_row, n_col, line_ref, docs_ref, level_one_ref, level_two_ref,
-    arrived, counts, whole_one, whole_two,
-    out_ref, cnt_ref, one_ref, two_ref,
+    inputs, targets, total, whole_one, whole_two,
+    arrived, counts, out_ref, cnt_ref, one_ref, two_ref,
     doc_send, doc_recv, cnt_send, cnt_recv, up_send, down_send, one_recv,
     pair_send, pair_recv, two_send, two_recv, local_sem,
 ):
@@ -67,6 +67,7 @@
     chips = n_col // 2
     place, core = col // 2, col % 2
     lines, width = arrived.shape[1:]
+    kept = inputs.shape[1]
     depth = docs_ref.shape[0]
     barrier = pltpu.get_barrier_semaphore()
 
@@ -135,8 +136,8 @@
     own[0].start()
     own[1].start()
 
-    path = lax.broadcasted_iota(jnp.int32, (n, 8, depth), 0) * lines
-    wide = jnp.broadcast_to(line_ref[...][None], (n, 8, depth))
+    path = lax.broadcasted_iota(jnp.int32, (n, 1, depth), 0) * lines
+    wide = jnp.broadcast_to(line_ref[...][None], (n, 1, depth))
     named = ((wide >= path) & (wide < path + lines)).astype(jnp.float32)
     cnt_ref[...] = jnp.broadcast_to(jnp.sum(named, axis=-1, keepdims=True), cnt_ref.shape)
 
@@ -208,8 +209,27 @@
             def _():
                 along(whole_one.at[high], high, col - 2, down_send).start()
 
+    def unpack(source):
+        rows = arrived[source].astype(jnp.float32)
+        inputs[source] = rows[:kept]
+        targets[source] = rows[lines - kept :]
+        total[...] += counts[source]
+
     for copy in own:
         copy.wait()
+    total[...] = jnp.zeros_like(total)
+    unpack(me)
+
+    for step in range(1, n_row + 1):
+        shift = step % n_row
+
+        def finish(turn, carry):
+            for copy in pair_of(shift, turn):
+                copy.wait()
+            unpack((row - shift + n_row) % n_row * n_col + (col - turn + n_col) % n_col)
+            return carry
+
+        lax.fori_loop(1 if shift == 0 else 0, n_col, finish, 0)
 
     for q in range(chips):
         block = 2 * q + core
@@ -227,17 +247,8 @@
     for k in range(1, n_row):
         two_copy(k).wait()
 
-    for shift in range(n_row):
-
-        def finish(turn, carry):
-            for copy in pair_of(shift, turn):
-                copy.wait()
-            return carry
-
-        lax.fori_loop(1 if shift == 0 else 0, n_col, finish, 0)
-
-
-def exchange(n_row, n_col, lines, line, docs, level_one, level_two):
+
+def exchange(n_row, n_col, lines, kept, line, docs, level_one, level_two):
     n = n_row * n_col
     width = docs.shape[-1]
     vmem = pl.BlockSpec(memory_space=pltpu.VMEM)
@@ -245,16 +256,19 @@
     return pl.pallas_call(
         functools.partial(exchange_kernel, n_row, n_col),
         out_shape=(
-            jax.ShapeDtypeStruct((n, lines, width), jnp.bfloat16),
-            jax.ShapeDtypeStruct((n, 8, 128), jnp.float32),
+            jax.ShapeDtypeStruct((n, kept, width), jnp.float32),
+            jax.ShapeDtypeStruct((n, kept, width), jnp.float32),
+            jax.ShapeDtypeStruct((1, 128), jnp.float32),
             jax.ShapeDtypeStruct((n_col,) + level_one.shape, jnp.bfloat16),
             jax.ShapeDtypeStruct((n_row,) + level_two.shape, jnp.bfloat16),
         ),
         in_specs=[vmem] * 4,
-        out_specs=(vmem,) * 4,
+        out_specs=(vmem,) * 5,
         scratch_shapes=[
             pltpu.VMEM((n, lines, width), jnp.bfloat16),
-            pltpu.VMEM((n, 8, 128), jnp.float32),
+            pltpu.VMEM((n, 1, 128), jnp.float32),
+            pltpu.VMEM((n, lines, width), jnp.bfloat16),
+            pltpu.VMEM((n, 1, 128), jnp.float32),
             pltpu.VMEM(level_one.shape, jnp.bfloat16),
             pltpu.VMEM(level_two.shape, jnp.bfloat16),
             dma((n,)), dma((n,)), dma((n,)), dma((n,)),
@@ -391,19 +405,19 @@
     rank = jnp.sum(same.astype(jnp.int32), axis=1)
     steps = jnp.arange(length, dtype=jnp.int32)
     line = ((target * length * capacity + rank)[:, None] + steps[None, :] * capacity).reshape(-1)
-    arrived, counts, whole_one, whole_two = exchange(
+    inputs, targets, filled, whole_one, whole_two = exchange(
         n_row,
         n_col,
         length * capacity,
+        (length - 1) * capacity,
         line[None, :],
         docs.reshape(count * length, width),
         level_one[0],
         level_two[0],
     )
-    total = jnp.sum(counts[:, 0, 0]) * ((length - 1) / length)
-    blocks = arrived.astype(jnp.float32)
-    inputs = blocks[:, : (length - 1) * capacity].reshape(-1, width)
-    targets = blocks[:, capacity:].reshape(-1, width)
+    total = filled[0, 0] * ((length - 1) / length)
+    inputs = inputs.reshape(-1, width)
+    targets = targets.reshape(-1, width)
     whole_one = whole_one.reshape(width, width).astype(jnp.float32)
     whole_two = whole_two.reshape(width, width).astype(jnp.float32)
     end_one, end_two = train_path(whole_one, whole_two, inputs, targets, total)

time: 144 us -> 140 us (0.972)
  other arithmetic: 10.2 us -> 8.46 us
    convert_element_type x1 -> x0, other arithmetic: 1.96 us -> none  [shards(): blocks = arrived.astype(jnp.float32)]
    reduce_sum x1, other arithmetic: 0.25 us -> 2.02 us  [normalize(): jnp.mean(values * values, axis=-1, keepdims=True) + 1e-06]
    reduce_sum x1 -> x0, other arithmetic: 1.54 us -> none  [shards(): total = jnp.sum(counts[:, 0, 0]) * ((length - 1) / length)]
where the time goes in v2:
time: 140 us
  Pallas kernels  88.9 us (64%)
  matrix products  36.3 us (26%)
  other arithmetic  8.46 us (6%)
  local copies, waits for them, and re-layouts  4.39 us (3%)
  between operations  1.7 us (1%)
    pallas_call x1, Pallas kernels, exchange(): pl.pallas_call(functools.partial(exchange_kernel, n_row, n_col), out_shap...  61.9 us
    pallas_call x1, Pallas kernels, scatter(): pl.pallas_call(functools.partial(scatter_kernel, n_row, n_col), out_shape...  26.9 us
    dot_general x9, matrix products, path_loss(): jnp.dot(normalize(hidden).astype(jnp.bfloat16), second.astype(jnp.bfloat1...  18.8 us
    dot_general x6, matrix products, path_loss(): jnp.dot(normalize(inputs).astype(jnp.bfloat16), first.astype(jnp.bfloat16...  17.5 us

profile of v2, /device:TPU:0, one launch (start us, length us, event | category | flops | bytes accessed | tf_op | source)
XLA Modules:
  0.0 139.7 jit_solution(11127128566230362309)
XLA Ops:
  0.6 0.9 convert_reduce_fusion
  1.5 0.7 fusion.123
  2.2 0.1 broadcast_add_fusion
  2.3 0.7 add.116.line_ref
  3.0 2.4 %reshape.135.docs_ref = bf16[512,896]{1,0:T(8,128)(2,1)} reshape(bf16[128,4,896]{2,1,0:T(4,128)(2,1)} %param.6) | data formatting | bytes 1835008 | tf_op jit(solution)/shard_map/reshape | solution.py:414
  5.4 61.9 %shard_map.93 = (f32[32,24,896]{2,1,0:T(8,128)}, f32[32,24,896]{2,1,0:T(8,128)}, f32[1,128]{1,0:T(1,128)}, bf16[8,112,896]{2,1,0:T(8,128)(2,1)}, bf16[4,224,896]{2,1,0:T(8,128)(2,1)}) custom-call(s32[1,512]{1,0:T(1,128)} %add.116.line_ref, bf16[512,896]{1,0:T(8,128)(2,1)} %reshape.135.docs_ref, f32[112,896]{1,0:T(8,128)} %bitcast.78, f32[224,896]{1,0:T(8,128)} %bitcast.75), custom_call_target="tpu_custom_call" | custom-call | tf_op jit(solution)/shard_map/pallas_call | solution.py:256
  67.3 0.0 copy-start.1
  68.2 2.0 %multiply_reduce_fusion.3 = f32[32,24]{1,0:T(8,128)S(1)} fusion(f32[32,24,896]{2,1,0:T(8,128)} %get-tuple-element.12), kind=kLoop, calls=%fused_computation.73 | loop fusion | flops 1375488 | bytes 2755584 | tf_op jit(solution)/shard_map/jvp()/reduce_sum | solution.py:21
  70.3 0.1 rsqrt.45
  70.3 0.0 copy-done.1
  70.4 0.0 copy-start.7
  70.4 0.2 multiply_convert_fusion.3
  70.6 1.2 copy-done.7
  71.8 0.0 copy-start
  71.8 0.0 copy-start.6
  71.8 2.4 %multiply_reduce_fusion.2 = (f32[768]{0:T(1024)S(1)}, f32[768,896]{1,0:T(8,128)S(1)}, bf16[768,896]{1,0:T(8,128)(2,1)S(1)}, f32[768,896]{1,0:T(8,128)S(1)}) fusion(f32[32,24,896]{2,1,0:T(8,128)S(1)} %copy-done.1, f32[768]{0:T(1024)S(1)} %rsqrt.45, bf16[768,896]{1,0:T(8,128)(2,1)S(1)} %bitcast.79, bf16[896,896]{1,0:T(8,128)(2,1)S(1)} %bitcast.80), kind=kOutput, calls=%fused_computation.70 | convolution fusion | flops 1240005888 | bytes 12621824 | tf_op jit(solution)/shard_map/jvp()/dot_general | solution.py:28
  74.2 0.0 copy-done
  74.2 0.0 copy-done.6
  74.3 1.8 %fusion.26 = f32[768,896]{1,0:T(8,128)S(1)} fusion(f32[32,24,896]{2,1,0:T(8,128)S(1)} %copy-done.6, f32[768,896]{1,0:T(8,128)S(1)} %get-tuple-element.27, bf16[896,896]{1,0:T(8,128)(2,1)S(1)} %bitcast.70, f32[]{:T(128)} %bitcast.10, f32[768]{0:T(1024)S(1)} %fusion.120), kind=kOutput, calls=%fused_computation.44 | convolution fusion | flops 1237942272 | bytes 9866244 | tf_op jit(solution)/shard_map/jvp()/dot_general | solution.py:38
  76.1 1.8 %fusion.5 = (f32[768]{0:T(1024)S(1)}, bf16[768,896]{1,0:T(8,128)(2,1)S(1)}) fusion(f32[768,896]{1,0:T(8,128)S(1)} %get-tuple-element.27, bf16[896,896]{1,0:T(8,128)(2,1)S(1)} %bitcast.71, f32[768,896]{1,0:T(8,128)S(1)} %fusion.26), kind=kOutput, calls=%fused_computation.23 | convolution fusion | flops 1236565248 | bytes 8489984 | tf_op jit(solution)/shard_map/transpose(jvp())/dot_general | solution.py:38
  78.0 2.8 %fusion.73 = bf16[896,896]{1,0:T(8,128)(2,1)S(1)} fusion(bf16[768,896]{1,0:T(8,128)(2,1)S(1)} %get-tuple-element.28, f32[768,896]{1,0:T(8,128)S(1)} %fusion.26, bf16[768,896]{1,0:T(8,128)(2,1)S(1)} %get-tuple-element.31, f32[768,896]{1,0:T(8,128)S(1)} %get-tuple-element.27, f32[768,896]{1,0:T(8,128)S(1)} %get-tuple-element.29, ...), kind=kOutput, calls=%fused_computation.96 | convolution fusion | flops 1245626368 | bytes 12621824 | tf_op jit(solution)/shard_map/transpose(jvp())/dot_general | solution.py:28
  80.7 1.7 %fusion.58 = bf16[896,896]{1,0:T(8,128)(2,1)S(1)} fusion(f32[768,896]{1,0:T(8,128)S(1)} %fusion.26, f32[768,896]{1,0:T(8,128)S(1)} %get-tuple-element.27, f32[768]{0:T(1024)S(1)} %fusion.120), kind=kOutput, calls=%fused_computation.91 | convolution fusion | flops 1235992576 | bytes 7113728 | tf_op jit(solution)/shard_map/transpose(jvp())/dot_general | solution.py:38
  82.5 2.5 %multiply_reduce_fusion.1 = (f32[768]{0:T(1024)S(1)}, f32[768,896]{1,0:T(8,128)S(1)}, f32[768,896]{1,0:T(8,128)S(1)}) fusion(f32[32,24,896]{2,1,0:T(8,128)S(1)} %copy-done.1, bf16[768,896]{1,0:T(8,128)(2,1)S(1)} %get-tuple-element.28, bf16[896,896]{1,0:T(8,128)(2,1)S(1)} %fusion.73, bf16[896,896]{1,0:T(8,128)(2,1)S(1)} %bitcast.81), kind=kOutput, calls=%fused_computation.64 | convolution fusion | flops 1242643712 | bytes 12848128 | tf_op jit(solution)/shard_map/jvp()/dot_general | solution.py:28
  85.0 1.9 %fusion.28 = f32[768,896]{1,0:T(8,128)S(1)} fusion(f32[32,24,896]{2,1,0:T(8,128)S(1)} %copy-done.6, f32[768,896]{1,0:T(8,128)S(1)} %get-tuple-element.25, f32[]{:T(128)} %bitcast.10, f32[768]{0:T(1024)S(1)} %fusion.121, bf16[896,896]{1,0:T(8,128)(2,1)S(1)} %fusion.58, bf16[896,896]{1,0:T(8,128)(2,1)S(1)} %bitcast.72), kind=kOutput, calls=%fused_computation.46 | convolution fusion | flops 1241956352 | bytes 11471876 | tf_op jit(solution)/shard_map/jvp()/dot_general | solution.py:38
  86.9 1.9 %fusion.7 = (f32[768]{0:T(1024)S(1)}, bf16[768,896]{1,0:T(8,128)(2,1)S(1)}) fusion(f32[768,896]{1,0:T(8,128)S(1)} %get-tuple-element.25, bf16[896,896]{1,0:T(8,128)(2,1)S(1)} %fusion.58, bf16[896,896]{1,0:T(8,128)(2,1)S(1)} %bitcast.73, f32[768,896]{1,0:T(8,128)S(1)} %fusion.28), kind=kOutput, calls=%fused_computation.25 | convolution fusion | flops 1240579328 | bytes 10095616 | tf_op jit(solution)/shard_map/transpose(jvp())/dot_general | solution.py:38
  88.8 2.8 %fusion.70 = bf16[896,896]{1,0:T(8,128)(2,1)S(1)} fusion(bf16[768,896]{1,0:T(8,128)(2,1)S(1)} %get-tuple-element.28, f32[768,896]{1,0:T(8,128)S(1)} %fusion.28, bf16[768,896]{1,0:T(8,128)(2,1)S(1)} %get-tuple-element.34, f32[768,896]{1,0:T(8,128)S(1)} %get-tuple-element.25, f32[768,896]{1,0:T(8,128)S(1)} %get-tuple-element.32, ...), kind=kOutput, calls=%fused_computation.95 | convolution fusion | flops 1245626368 | bytes 12621824 | tf_op jit(solution)/shard_map/transpose(jvp())/dot_general | solution.py:28
  91.6 2.1 %fusion.57 = (bf16[896,896]{1,0:T(8,128)(2,1)S(1)}, bf16[896,896]{1,0:T(8,128)(2,1)S(1)}) fusion(bf16[896,896]{1,0:T(8,128)(2,1)S(1)} %fusion.58, bf16[4,224,896]{2,1,0:T(8,128)(2,1)S(1)} %copy-done, f32[768,896]{1,0:T(8,128)S(1)} %fusion.28, f32[768,896]{1,0:T(8,128)S(1)} %get-tuple-element.25, f32[768]{0:T(1024)S(1)} %fusion.121), kind=kOutput, calls=%fused_computation.90 | convolution fusion | flops 1242415104 | bytes 11930624 | tf_op jit(solution)/shard_map/transpose(jvp())/dot_general | solution.py:38
  93.7 2.4 %multiply_reduce_fusion = (f32[768]{0:T(1024)S(1)}, f32[768,896]{1,0:T(8,128)S(1)}, f32[768,896]{1,0:T(8,128)S(1)}) fusion(f32[32,24,896]{2,1,0:T(8,128)S(1)} %copy-done.1, bf16[768,896]{1,0:T(8,128)(2,1)S(1)} %get-tuple-element.28, bf16[896,896]{1,0:T(8,128)(2,1)S(1)} %fusion.70, bf16[896,896]{1,0:T(8,128)(2,1)S(1)} %fusion.73, ...), kind=kOutput, calls=%fused_computation.58 | convolution fusion | flops 1245052160 | bytes 14453760 | tf_op jit(solution)/shard_map/jvp()/dot_general | solution.py:28
  96.1 1.8 %fusion.30 = f32[768,896]{1,0:T(8,128)S(1)} fusion(f32[32,24,896]{2,1,0:T(8,128)S(1)} %copy-done.6, f32[768,896]{1,0:T(8,128)S(1)} %get-tuple-element.23, bf16[896,896]{1,0:T(8,128)(2,1)S(1)} %get-tuple-element.36, f32[]{:T(128)} %bitcast.10, f32[768]{0:T(1024)S(1)} %fusion.122), kind=kOutput, calls=%fused_computation.48 | convolution fusion | flops 1237942272 | bytes 9866244 | tf_op jit(solution)/shard_map/jvp()/dot_general | solution.py:38
  97.9 3.9 %fusion.1 = bf16[896,896]{1,0:T(8,128)(2,1)} fusion(bf16[896,896]{1,0:T(8,128)(2,1)S(1)} %bitcast.74, bf16[896,896]{1,0:T(8,128)(2,1)S(1)} %get-tuple-element.37, bf16[896,896]{1,0:T(8,128)(2,1)S(1)} %fusion.58, f32[768,896]{1,0:T(8,128)S(1)} %fusion.30, f32[768,896]{1,0:T(8,128)S(1)} %get-tuple-element.23, f32[768]{0:T(1024)S(1)} %fusion.122), kind=kOutput, calls=%fused_computation.17 | convolution fusion | flops 1245626368 | bytes 11930624 | tf_op jit(solution)/shard_map/transpose(jvp())/dot_general | solution.py:38
  101.8 1.8 %fusion.9 = (f32[768]{0:T(1024)S(1)}, bf16[768,896]{1,0:T(8,128)(2,1)S(1)}) fusion(f32[768,896]{1,0:T(8,128)S(1)} %get-tuple-element.23, bf16[896,896]{1,0:T(8,128)(2,1)S(1)} %get-tuple-element.36, f32[768,896]{1,0:T(8,128)S(1)} %fusion.30), kind=kOutput, calls=%fused_computation.27 | convolution fusion | flops 1236565248 | bytes 8489984 | tf_op jit(solution)/shard_map/transpose(jvp())/dot_general | solution.py:38
  103.7 4.6 %fusion = bf16[896,896]{1,0:T(8,128)(2,1)} fusion(bf16[896,896]{1,0:T(8,128)(2,1)S(1)} %bitcast.83, bf16[896,896]{1,0:T(8,128)(2,1)S(1)} %fusion.70, bf16[896,896]{1,0:T(8,128)(2,1)S(1)} %fusion.73, bf16[768,896]{1,0:T(8,128)(2,1)S(1)} %get-tuple-element.28, f32[768,896]{1,0:T(8,128)S(1)} %fusion.30, bf16[768,896]{1,0:T(8,128)(2,1)S(1)} %get-tuple-element.39, ...), kind=kOutput, calls=%fused_computation.16 | convolution fusion | flops 1255260160 | bytes 17438720 | tf_op jit(solution)/shard_map/transpose(jvp())/dot_general | solution.py:28
  108.3 0.0 copy-start.3
  108.3 0.0 copy-start.5
  108.3 0.0 copy-start.2
  108.3 0.0 copy-start.4
  108.3 26.9 %shard_map.94 = (f32[112,896]{1,0:T(8,128)}, f32[224,896]{1,0:T(8,128)}) custom-call(bf16[8,112,896]{2,1,0:T(8,128)(2,1)} %bitcast.77, bf16[4,224,896]{2,1,0:T(8,128)(2,1)} %bitcast.76), custom_call_target="tpu_custom_call" | custom-call | tf_op jit(solution)/shard_map/pallas_call | solution.py:371
  135.2 0.0 copy-done.3
  135.2 0.0 copy-done.5
  135.2 2.0 %fusion.118 = (f32[1,112,896]{2,1,0:T(8,128)}, f32[1,112,896]{2,1,0:T(8,128)}) fusion(f32[1,112,896]{2,1,0:T(8,128)S(1)} %copy-done.3, f32[112,896]{1,0:T(8,128)} %get-tuple-element.16, f32[1,112,896]{2,1,0:T(8,128)S(1)} %copy-done.5), kind=kLoop, calls=%fused_computation.129 | loop fusion | flops 702464 | bytes 2007040 | tf_op jit(solution)/shard_map/sub | solution.py:434
  137.2 0.0 copy-done.2
  137.2 0.0 copy-done.4
  137.2 2.5 %fusion.114 = (f32[1,224,896]{2,1,0:T(8,128)}, f32[1,224,896]{2,1,0:T(8,128)}) fusion(f32[1,224,896]{2,1,0:T(8,128)S(1)} %copy-done.2, f32[224,896]{1,0:T(8,128)} %get-tuple-element.17, f32[1,224,896]{2,1,0:T(8,128)S(1)} %copy-done.4), kind=kLoop, calls=%fused_computation.125 | loop fusion | flops 1404928 | bytes 4014080 | tf_op jit(solution)/shard_map/sub | solution.py:435
  (8 shorter events, 0.1 us)
Async XLA Ops:
  67.3 3.0 %copy-start.1 = (f32[32,24,896]{2,1,0:T(8,128)S(1)}, f32[32,24,896]{2,1,0:T(8,128)}, u32[]{:S(2)}) copy-start(f32[32,24,896]{2,1,0:T(8,128)} %get-tuple-element.12) | copy-start | bytes 8257540
  70.4 1.4 %copy-start.7 = (bf16[8,112,896]{2,1,0:T(8,128)(2,1)S(1)}, bf16[8,112,896]{2,1,0:T(8,128)(2,1)}, u32[]{:S(2)}) copy-start(bf16[8,112,896]{2,1,0:T(8,128)(2,1)} %get-tuple-element.11) | copy-start | bytes 4816900
  71.8 2.5 %copy-start = (bf16[4,224,896]{2,1,0:T(8,128)(2,1)S(1)}, bf16[4,224,896]{2,1,0:T(8,128)(2,1)}, u32[]{:S(2)}) copy-start(bf16[4,224,896]{2,1,0:T(8,128)(2,1)} %get-tuple-element.13) | copy-start | bytes 4816900
  71.8 2.5 %copy-start.6 = (f32[32,24,896]{2,1,0:T(8,128)S(1)}, f32[32,24,896]{2,1,0:T(8,128)}, u32[]{:S(2)}) copy-start(f32[32,24,896]{2,1,0:T(8,128)} %get-tuple-element.14) | copy-start | bytes 8257540
  108.3 26.9 %copy-start.3 = (f32[1,112,896]{2,1,0:T(8,128)S(1)}, f32[1,112,896]{2,1,0:T(8,128)}, u32[]{:S(2)}) copy-start(f32[1,112,896]{2,1,0:T(8,128)} %param.8) | copy-start | bytes 1204228
  108.3 27.0 %copy-start.5 = (f32[1,112,896]{2,1,0:T(8,128)S(1)}, f32[1,112,896]{2,1,0:T(8,128)}, u32[]{:S(2)}) copy-start(f32[1,112,896]{2,1,0:T(8,128)} %param.10) | copy-start | bytes 1204228
  108.3 29.0 %copy-start.2 = (f32[1,224,896]{2,1,0:T(8,128)S(1)}, f32[1,224,896]{2,1,0:T(8,128)}, u32[]{:S(2)}) copy-start(f32[1,224,896]{2,1,0:T(8,128)} %param.9) | copy-start | bytes 2408452
  108.3 29.0 %copy-start.4 = (f32[1,224,896]{2,1,0:T(8,128)S(1)}, f32[1,224,896]{2,1,0:T(8,128)}, u32[]{:S(2)}) copy-start(f32[1,224,896]{2,1,0:T(8,128)} %param.11) | copy-start | bytes 2408452
